TPU v7x, 16 devices: a 4x2x1 block of a 4x4x8 slice. The times are simulated.
16 devices in a mesh: dp: 2 (over y, z), fsdp: 8 (over x, core).
Axes of the slice: x: 4, y: 2, z: 1, core: 2. Of those that a mesh axis runs over, the one named last changes fastest.
The devices are a block of a 4x4x8 slice.
Arguments:
- x: bfloat16 [16, 1024, 2048], P(('dp', 'fsdp')), parts along dimension 0
- gain: bfloat16 [2, 2048], replicated
- w_in: bfloat16 [2, 2048, 18944], P(None, None, 'fsdp')
- w_out: bfloat16 [2, 10240, 2048], P(None, 'fsdp')
Outputs:
- output 1: bfloat16 [16, 1024, 2048], P(('dp', 'fsdp')), parts along dimension 0
- output 2: bfloat16 [2, 16, 1024, 256], P(None, ('dp', 'fsdp')), parts along dimension 1
- output 3: bfloat16 [2, 16, 1024, 256], P(None, ('dp', 'fsdp')), parts along dimension 1
There are 2 independent parts. A program takes and returns all parts, laid end to end along the dimension named above; an argument that names none is the same for every part.
All inputs are finite; a program needn't handle non-finite values.
Results may differ from a plain program's by a relative error of at most 0.012933.
Values are sent between devices in bfloat16 or wider.
A program may use at most 768 MiB of HBM per device.

v0:
```python
import jax
import jax.numpy as jnp
from jax import lax
from jax.sharding import PartitionSpec as P

HEAD_DIM = 256
ROPE_BASE = 10000.0
NORM_EPS = 1e-6


def layer_norm(hidden, gain_vec):
    x_float = hidden.astype(jnp.float32)
    centred = x_float - jnp.mean(x_float, axis=-1, keepdims=True)
    variance = jnp.mean(centred * centred, axis=-1, keepdims=True)
    return (centred * lax.rsqrt(variance + NORM_EPS) * gain_vec.astype(jnp.float32)).astype(jnp.bfloat16)


def rope_tables(seq_len):
    half_dim = HEAD_DIM // 2
    inv_freq = ROPE_BASE ** (-jnp.arange(half_dim, dtype=jnp.float32) / half_dim)
    angle = jnp.arange(seq_len, dtype=jnp.float32)[:, None] * inv_freq[None, :]
    return jnp.cos(angle), jnp.sin(angle)


def apply_rope(tensor, cos_table, sin_table):
    half_dim = HEAD_DIM // 2
    first = tensor[..., :half_dim]
    second = tensor[..., half_dim:]
    return jnp.concatenate([first * cos_table - second * sin_table, second * cos_table + first * sin_table], axis=-1)


def mix_tokens(projected, num_heads, ff_dim):
    batch, seq_len, _ = projected.shape
    q_cols = num_heads * HEAD_DIM
    query = projected[..., :q_cols].reshape(batch, seq_len, num_heads, HEAD_DIM)
    key_raw = projected[..., q_cols:q_cols + HEAD_DIM]
    value = projected[..., q_cols + HEAD_DIM:q_cols + 2 * HEAD_DIM]
    gate = projected[..., q_cols + 2 * HEAD_DIM:q_cols + 2 * HEAD_DIM + ff_dim]
    up_proj = projected[..., q_cols + 2 * HEAD_DIM + ff_dim:]
    cos_table, sin_table = rope_tables(seq_len)
    q_rot = (apply_rope(query.astype(jnp.float32), cos_table[:, None, :], sin_table[:, None, :]) * HEAD_DIM ** -0.5).astype(jnp.bfloat16)
    k_rot = apply_rope(key_raw.astype(jnp.float32), cos_table, sin_table).astype(jnp.bfloat16)
    scores = jnp.einsum("crie,cle->cril", q_rot, k_rot, preferred_element_type=jnp.float32)
    causal = jnp.arange(seq_len)[:, None, None] >= jnp.arange(seq_len)[None, None, :]
    scores = jnp.where(causal, scores, -1e30)
    exp_scores = jnp.exp(scores - jnp.max(scores, axis=-1, keepdims=True))
    row_sum = jnp.sum(exp_scores, axis=-1, keepdims=True)
    attended = jnp.einsum("cril,cle->crie", exp_scores.astype(jnp.bfloat16), value, preferred_element_type=jnp.float32) / row_sum
    attended = attended.astype(jnp.bfloat16).reshape(batch, seq_len, q_cols)
    gated = (jax.nn.silu(gate.astype(jnp.float32)) * up_proj.astype(jnp.float32)).astype(jnp.bfloat16)
    return attended, gated, k_rot, value


def parallel_layer(hidden, gain_vec, w_in_full, w_out_full):
    out_rows = w_out_full.shape[0]
    ff_dim = w_in_full.shape[1] - out_rows - 2 * HEAD_DIM
    num_heads = (out_rows - ff_dim) // HEAD_DIM
    q_cols = num_heads * HEAD_DIM
    normed = layer_norm(hidden, gain_vec)
    projected = jnp.einsum("bsd,de->bse", normed, w_in_full, preferred_element_type=jnp.float32).astype(jnp.bfloat16)
    attended, gated, k_rot, value = mix_tokens(projected, num_heads, ff_dim)
    out_sum = jnp.einsum("bsr,rd->bsd", attended, w_out_full[:q_cols], preferred_element_type=jnp.float32)
    out_sum = out_sum + jnp.einsum("bsf,fd->bsd", gated, w_out_full[q_cols:], preferred_element_type=jnp.float32)
    new_hidden = (hidden.astype(jnp.float32) + out_sum).astype(jnp.bfloat16)
    return new_hidden, k_rot, value


def solution(mesh):
    batch_axes = ("dp", "fsdp")

    def device_program(x_local, gain, w_in_local, w_out_local):
        hidden = x_local
        key_list = []
        value_list = []
        for layer in range(w_in_local.shape[0]):
            w_in_full = lax.all_gather(w_in_local[layer], "fsdp", axis=1, tiled=True)
            w_out_full = lax.all_gather(w_out_local[layer], "fsdp", axis=0, tiled=True)
            hidden, k_rot, value = parallel_layer(hidden, gain[layer], w_in_full, w_out_full)
            key_list.append(k_rot)
            value_list.append(value)
        return hidden, jnp.stack(key_list), jnp.stack(value_list)

    return jax.shard_map(
        device_program,
        mesh=mesh,
        in_specs=(P(batch_axes, None, None), P(None, None), P(None, None, "fsdp"), P(None, "fsdp", None)),
        out_specs=(P(batch_axes, None, None), P(None, batch_axes, None, None), P(None, batch_axes, None, None)),
        check_vma=False,
    )
```

profile of v0, /device:TPU:113, one launch (start us, length us, event | category | flops | bytes accessed | tf_op | source)
XLA Modules:
  0.0 1149.2 jit_solution(13530657813824965533)
XLA Ops:
  7.2 0.1 all-gather.9.cloned.1.call-start
  7.2 15.5 %fusion.92 = (bf16[1,2048,2368]{1,2,0:T(8,128)(2,1)}, bf16[1,2048,2368]{1,2,0:T(8,128)(2,1)}) fusion(bf16[2,2048,2368]{1,2,0:T(8,128)(2,1)} %param.6), kind=kLoop, calls=%fused_computation.132 | loop fusion | bytes 38797312 | tf_op jit(solution)/shard_map/slice | solution.py:76
  22.8 0.1 all-gather.11.cloned.1.call-start
  22.9 10.2 fusion.93
  33.1 0.1 all-gather.13.cloned.1.call-start
  33.2 0.7 all-gather.13.cloned.1.call-update
  33.9 0.1 all-gather.15.cloned.1.call-start
  34.0 0.6 all-gather.15.cloned.1.call-update
  34.6 1.3 iota_compare_fusion
  35.8 2.8 convert_reduce_fusion.1
  38.7 3.4 fusion.45
  42.1 3.1 fusion.79
  45.2 0.6 slice_convert_fusion.4
  45.8 319.3 %all-gather.9.cloned.1.call-done = bf16[1,2048,18944]{1,2,0:T(8,128)(2,1)} async-done(((bf16[1,2048,2368]{1,2,0:T(8,128)(2,1)}), bf16[1,2048,18944]{1,2,0:T(8,128)(2,1)}) %all-gather.9.cloned.1.call-update) | async-done | bytes 77594640 | tf_op jit(solution)/shard_map/all_gather | solution.py:76
  365.1 93.0 %convert_bitcast_fusion.1 = bf16[1,1024,18944]{2,1,0:T(8,128)(2,1)} fusion(bf16[1,2048,18944]{1,2,0:T(8,128)(2,1)} %all-gather.9.cloned.1.call-done, bf16[1,1024,2048]{2,1,0:T(8,128)(2,1)} %param.4, f32[2048]{0:T(1024)S(1)} %bitcast.129, f32[1024]{0:T(1024)S(1)} %add_rsqrt_fusion.1, f32[1024]{0:T(1024)S(1)} %broadcast_multiply_fusion.1), kind=kOutput, calls=%fused_computation.9 | convolution fusion | flops 79486779392 | bytes 120602624 | tf_op jit(solution)/shard_map/bsd,de->bse/dot_general | solution.py:60
  458.0 3.2 slice_convert_fusion.1
  461.3 4.1 copy.25
  465.4 2.1 slice_bitcast_fusion.13
  467.5 2.4 subtract_convert_fusion.1
  469.9 0.5 fusion.95
  470.5 0.7 copy-done.3
  471.2 0.2 copy-done.5
  471.3 4.9 subtract_bitcast_fusion.1
  476.2 17.1 %select_reduce_fusion.1 = (f32[1024,8]{0,1:T(8,128)S(1)}, f32[1024,8,1024]{0,2,1:T(8,128)}) fusion(pred[1024,1024]{0,1:T(8,128)(4,1)S(1)} %copy-done.1, bf16[1024,128]{1,0:T(8,128)(2,1)S(1)} %bitcast.122, bf16[1024,128]{1,0:T(8,128)(2,1)S(1)} %bitcast.120, f32[1024,8,128]{2,0,1:T(8,128)} %get-tuple-element.14, f32[1024,8,128]{2,0,1:T(8,128)} %get-tuple-element.13), kind=kOutput, calls=%fused_computation.27 | convolution fusion | flops 4319076352 | bytes 43548672 | tf_op jit(solution)/shard_map/crie,cle->cril/dot_general | solution.py:43
  493.4 13.7 %fusion.20 = f32[1024,8]{0,1:T(8,128)S(1)} fusion(f32[1024,8,1024]{0,2,1:T(8,128)} %get-tuple-element.28, f32[1024,8]{0,1:T(8,128)S(1)} %get-tuple-element.27, pred[1024,1024]{0,1:T(8,128)(4,1)S(1)} %copy-done.1), kind=kLoop, calls=%fused_computation.28 | loop fusion | flops 25157632 | bytes 34668544 | tf_op jit(solution)/shard_map/reduce_sum | solution.py:47
  507.1 16.0 %divide_convert_fusion.1 = bf16[1024,8,256]{0,2,1:T(8,128)(2,1)} fusion(f32[1024,8]{0,1:T(8,128)S(1)} %fusion.20, bf16[1,1024,18944]{2,1,0:T(8,128)(2,1)} %convert_bitcast_fusion.1, f32[1024,8,1024]{0,2,1:T(8,128)} %get-tuple-element.28, f32[1024,8]{0,1:T(8,128)S(1)} %get-tuple-element.27, pred[1024,1024]{0,1:T(8,128)(4,1)S(1)} %copy-done.1), kind=kOutput, calls=%fused_computation.69 | convolution fusion | flops 4324327424 | bytes 39387136 | tf_op jit(solution)/shard_map/cril,cle->crie/dot_general | solution.py:48
  523.1 32.0 %all-gather.11.cloned.1.call-done = bf16[1,10240,2048]{2,1,0:T(8,128)(2,1)} async-done(((bf16[1,1280,2048]{2,1,0:T(8,128)(2,1)}), bf16[1,10240,2048]{2,1,0:T(8,128)(2,1)}) %all-gather.11.cloned.1.call-update) | async-done | bytes 41943056 | tf_op jit(solution)/shard_map/all_gather | solution.py:77
  555.0 46.4 %fusion.17 = f32[1024,2048]{1,0:T(8,128)} fusion(bf16[1,10240,2048]{2,1,0:T(8,128)(2,1)} %all-gather.11.cloned.1.call-done, bf16[1,1024,18944]{2,1,0:T(8,128)(2,1)} %convert_bitcast_fusion.1), kind=kOutput, calls=%fused_computation.21 | convolution fusion | flops 34426847232 | bytes 75497472 | tf_op jit(solution)/shard_map/bsf,fd->bsd/dot_general | solution.py:63
  601.5 13.9 %convert_reduce_fusion = (f32[1024]{0:T(1024)S(1)}, bf16[1,1024,2048]{2,1,0:T(8,128)(2,1)S(1)}) fusion(f32[1024,2048]{1,0:T(8,128)} %fusion.17, bf16[1024,2048]{0,1:T(8,128)(2,1)S(1)} %bitcast.130, bf16[1,10240,2048]{2,1,0:T(8,128)(2,1)} %all-gather.11.cloned.1.call-done, bf16[1,1024,2048]{2,1,0:T(8,128)(2,1)S(1)} %copy-done), kind=kOutput, calls=%fused_computation.44 | convolution fusion | flops 8602516480 | bytes 29364224 | tf_op jit(solution)/shard_map/bsr,rd->bsd/dot_general | solution.py:62
  615.4 2.0 copy-done.7
  617.4 1.2 fusion.42
  618.7 276.1 %all-gather.13.cloned.1.call-done = bf16[1,2048,18944]{1,2,0:T(8,128)(2,1)} async-done(((bf16[1,2048,2368]{1,2,0:T(8,128)(2,1)}), bf16[1,2048,18944]{1,2,0:T(8,128)(2,1)}) %all-gather.13.cloned.1.call-update) | async-done | bytes 77594640 | tf_op jit(solution)/shard_map/all_gather | solution.py:76
  894.7 93.2 %convert_bitcast_fusion = bf16[1,1024,18944]{2,1,0:T(8,128)(2,1)} fusion(bf16[1,2048,18944]{1,2,0:T(8,128)(2,1)} %all-gather.13.cloned.1.call-done, bf16[1,1024,2048]{2,1,0:T(8,128)(2,1)} %copy-done.7, f32[2048]{0:T(1024)S(1)} %bitcast.128, f32[1024]{0:T(1024)S(1)} %add_rsqrt_fusion, f32[1024]{0:T(1024)S(1)} %broadcast_multiply_fusion), kind=kOutput, calls=%fused_computation.8 | convolution fusion | flops 79486779392 | bytes 120602624 | tf_op jit(solution)/shard_map/bsd,de->bse/dot_general | solution.py:60
  987.9 3.2 slice_convert_fusion
  991.2 4.1 copy.26
  995.3 1.3 slice_bitcast_fusion.12
  996.6 2.4 subtract_convert_fusion
  999.1 1.5 maximum_maximum_fusion
  1000.6 0.5 fusion.94
  1001.1 0.5 copy-done.4
  1001.6 0.2 copy-done.6
  1001.8 4.7 subtract_bitcast_fusion
  1006.5 17.0 %select_reduce_fusion = (f32[1024,8]{0,1:T(8,128)S(1)}, f32[1024,8,1024]{0,2,1:T(8,128)}) fusion(pred[1024,1024]{0,1:T(8,128)(4,1)S(1)} %copy-done.2, bf16[1024,128]{1,0:T(8,128)(2,1)S(1)} %bitcast.127, bf16[1024,128]{1,0:T(8,128)(2,1)S(1)} %bitcast.125, f32[1024,8,128]{2,0,1:T(8,128)} %get-tuple-element.12, f32[1024,8,128]{2,0,1:T(8,128)} %get-tuple-element.11), kind=kOutput, calls=%fused_computation.26 | convolution fusion | flops 4319076352 | bytes 43548672 | tf_op jit(solution)/shard_map/crie,cle->cril/dot_general | solution.py:43
  1023.5 13.7 %fusion.22 = f32[1024,8]{0,1:T(8,128)S(1)} fusion(f32[1024,8,1024]{0,2,1:T(8,128)} %get-tuple-element.32, f32[1024,8]{0,1:T(8,128)S(1)} %get-tuple-element.31, pred[1024,1024]{0,1:T(8,128)(4,1)S(1)} %copy-done.2), kind=kLoop, calls=%fused_computation.30 | loop fusion | flops 25157632 | bytes 34668544 | tf_op jit(solution)/shard_map/reduce_sum | solution.py:47
  1037.3 16.1 %divide_convert_fusion = bf16[1024,8,256]{0,2,1:T(8,128)(2,1)} fusion(f32[1024,8]{0,1:T(8,128)S(1)} %fusion.22, bf16[1,1024,18944]{2,1,0:T(8,128)(2,1)} %convert_bitcast_fusion, f32[1024,8,1024]{0,2,1:T(8,128)} %get-tuple-element.32, f32[1024,8]{0,1:T(8,128)S(1)} %get-tuple-element.31, pred[1024,1024]{0,1:T(8,128)(4,1)S(1)} %copy-done.2), kind=kOutput, calls=%fused_computation.68 | convolution fusion | flops 4324327424 | bytes 39387136 | tf_op jit(solution)/shard_map/cril,cle->crie/dot_general | solution.py:48
  1053.3 31.2 %all-gather.15.cloned.1.call-done = bf16[1,10240,2048]{2,1,0:T(8,128)(2,1)} async-done(((bf16[1,1280,2048]{2,1,0:T(8,128)(2,1)}), bf16[1,10240,2048]{2,1,0:T(8,128)(2,1)}) %all-gather.15.cloned.1.call-update) | async-done | bytes 41943056 | tf_op jit(solution)/shard_map/all_gather | solution.py:77
  1084.6 44.1 %fusion.16 = f32[1024,2048]{1,0:T(8,128)S(1)} fusion(bf16[1,10240,2048]{2,1,0:T(8,128)(2,1)} %all-gather.15.cloned.1.call-done, bf16[1,1024,18944]{2,1,0:T(8,128)(2,1)} %convert_bitcast_fusion), kind=kOutput, calls=%fused_computation.19 | convolution fusion | flops 34426847232 | bytes 75497472 | tf_op jit(solution)/shard_map/bsf,fd->bsd/dot_general | solution.py:63
  1128.7 13.7 %fusion.49 = bf16[1,1024,2048]{2,1,0:T(8,128)(2,1)} fusion(bf16[1,1024,2048]{2,1,0:T(8,128)(2,1)S(1)} %copy-done.8, f32[1024,2048]{1,0:T(8,128)S(1)} %fusion.16, bf16[1024,2048]{0,1:T(8,128)(2,1)S(1)} %bitcast.131, bf16[1,10240,2048]{2,1,0:T(8,128)(2,1)} %all-gather.15.cloned.1.call-done), kind=kOutput, calls=%fused_computation.59 | convolution fusion | flops 8598323200 | bytes 29360128 | tf_op jit(solution)/shard_map/bsr,rd->bsd/dot_general | solution.py:62
  (44 shorter events, 0.2 us)
Async XLA Ops:
  7.2 357.9 %all-gather.9.cloned.1.call-start = ((), (), s32[]{:S(2)}) async-start(), calls=%async_computation | async-start | bytes 87293952 | tf_op jit(solution)/shard_map/all_gather | solution.py:76
  22.8 532.2 %all-gather.11.cloned.1.call-start = ((), (), s32[]{:S(2)}) async-start(), calls=%async_computation.1 | async-start | bytes 47185920 | tf_op jit(solution)/shard_map/all_gather | solution.py:77
  33.1 861.6 %all-gather.13.cloned.1.call-start = ((), (), s32[]{:S(2)}) async-start(), calls=%async_computation.2 | async-start | bytes 87293952 | tf_op jit(solution)/shard_map/all_gather | solution.py:76
  33.9 11.3 copy-start.14
  33.9 1050.7 %all-gather.15.cloned.1.call-start = ((), (), s32[]{:S(2)}) async-start(), calls=%async_computation.3 | async-start | bytes 47185920 | tf_op jit(solution)/shard_map/all_gather | solution.py:77
  34.6 7.5 copy-start.16
  461.3 6.2 copy-start.17
  469.9 6.3 copy-start.10
  469.9 6.3 copy-start.12
  469.9 1.2 copy-start.3
  469.9 1.4 copy-start.5
  471.3 4.9 copy-start.1
  555.0 46.4 %copy-start = (bf16[1,1024,2048]{2,1,0:T(8,128)(2,1)S(1)}, bf16[1,1024,2048]{2,1,0:T(8,128)(2,1)}, u32[]{:S(2)}) copy-start(bf16[1,1024,2048]{2,1,0:T(8,128)(2,1)} %param.4) | copy-start | bytes 12582916
  555.0 46.4 %copy-start.19 = (bf16[1024,8,256]{0,2,1:T(8,128)(2,1)S(1)}, bf16[1024,8,256]{0,2,1:T(8,128)(2,1)}, u32[]{:S(2)}) copy-start(bf16[1024,8,256]{0,2,1:T(8,128)(2,1)} %divide_convert_fusion.1) | copy-start | bytes 12582916
  601.5 293.3 %copy-start.15 = (f32[1,2048]{1,0:T(1,128)S(1)}, f32[1,2048]{1,0:T(1,128)}, u32[]{:S(2)}) copy-start(f32[1,2048]{1,0:T(1,128)} %get-tuple-element.23) | copy-start | bytes 24580
  615.4 2.0 copy-start.7
  991.1 5.5 copy-start.18
  991.1 7.9 copy-start.9
  991.2 7.9 copy-start.11
  991.2 7.9 copy-start.13
  1000.6 1.0 copy-start.4
  1000.6 1.2 copy-start.6
  1001.8 4.7 copy-start.2
  1084.6 44.1 %copy-start.8 = (bf16[1,1024,2048]{2,1,0:T(8,128)(2,1)S(1)}, bf16[1,1024,2048]{2,1,0:T(8,128)(2,1)}, u32[]{:S(2)}) copy-start(bf16[1,1024,2048]{2,1,0:T(8,128)(2,1)} %copy-done.7) | copy-start | bytes 12582916
  1084.6 44.1 %copy-start.20 = (bf16[1024,8,256]{0,2,1:T(8,128)(2,1)S(1)}, bf16[1024,8,256]{0,2,1:T(8,128)(2,1)}, u32[]{:S(2)}) copy-start(bf16[1024,8,256]{0,2,1:T(8,128)(2,1)} %divide_convert_fusion) | copy-start | bytes 12582916
Sparse Core Ops, SparseCore 0:
  22.9 342.0 all-gather.8
  366.6 188.3 all-gather.10
  556.6 338.0 all-gather.12
  896.2 188.3 all-gather.14
where the time goes:
time: 1150 us
  waiting for transfers between devices  660 us (57%)
  matrix products  370 us (32%)
  other arithmetic  65.6 us (6%)
  local copies, waits for them, and re-layouts  38.5 us (3%)
  between operations  14.4 us (1%)
    all_gather x2, waiting for transfers between devices, device_program(): w_in_full = lax.all_gather(w_in_local[layer], 'fsdp', axis=1, tiled=True)  595 us
    dot_general x2, matrix products, parallel_layer(): jnp.einsum('bsd,de->bse', normed, w_in_full, preferred_element_type=jnp.f...  186 us
    dot_general x2, matrix products, parallel_layer(): jnp.einsum('bsf,fd->bsd', gated, w_out_full[q_cols:], preferred_element_t...  90.5 us
    all_gather x2, waiting for transfers between devices, device_program(): w_out_full = lax.all_gather(w_out_local[layer], 'fsdp', axis=0, tiled=True)  63.2 us
    dot_general x2, matrix products, mix_tokens(): jnp.einsum('crie,cle->cril', q_rot, k_rot, preferred_element_type=jnp.flo...  34.1 us
    dot_general x2, matrix products, mix_tokens(): jnp.einsum('cril,cle->crie', exp_scores.astype(jnp.bfloat16), value, pref...  32.1 us
    dot_general x2, matrix products, parallel_layer(): jnp.einsum('bsr,rd->bsd', attended, w_out_full[:q_cols], preferred_elemen...  27.6 us
    reduce_sum x2, other arithmetic, mix_tokens(): row_sum = jnp.sum(exp_scores, axis=-1, keepdims=True)  27.4 us
  transfers between devices with their start and end apart: 4, of which 4 were waited for; matrix products, arithmetic and copies ran while one was open for 35% of the time, Pallas kernels for 0%

commit v1 on v0

v1 whole, which is shorter than its diff:
```python
import functools

import jax
import jax.numpy as jnp
import numpy as np
from jax import lax
from jax.experimental import pallas as pl
from jax.experimental.pallas import tpu as pltpu
from jax.sharding import PartitionSpec as P

HEAD_DIM = 256
ROPE_BASE = 10000.0
NORM_EPS = 1e-6
MESH = pl.DeviceIdType.MESH
TILE = 512
ROWS = 512
CHUNKS = 4
AHEAD = 4


def rope_tables(seq_len):
    half = HEAD_DIM // 2
    angle = np.arange(seq_len)[:, None] * ROPE_BASE ** (-np.arange(half) / half)
    return np.cos(angle).astype(np.float32), np.sin(angle).astype(np.float32)


def part_rows(rows):
    step = 8 * CHUNKS
    outer = rows // (3 * step) * step
    return outer, rows - 2 * outer


def aligned(value, step):
    return pl.multiple_of(value, step)


def loop(lo, hi, body):
    lax.fori_loop(lo, hi, lambda i, c: (body(i), c)[1], 0)


def kernel(
    groups, group, x_ref, gain_ref, cos_ref, sin_ref, w_in_ref, w_out_ref,
    y_ref, k_ref, v_ref, g_in, g_out,
    h, acc, proj, kbuf, vbuf, wbuf, wtail,
    rx, rm, rp, rd, send, sd, wsem, tsem, ysem, kvsem,
):
    layers, width, cols = w_in_ref.shape
    out_rows = w_out_ref.shape[1]
    seq = x_ref.shape[1]
    rows_total = out_rows * group
    ff = cols * group - rows_total - 2 * HEAD_DIM
    q_cols = rows_total - ff
    heads = q_cols // HEAD_DIM
    chips = group // 2
    n_full = cols // TILE
    tail = cols - n_full * TILE
    half = HEAD_DIM // 2
    items = 3 * CHUNKS
    total = items * 2 * layers

    dp = lax.axis_index("dp")
    me = lax.axis_index("fsdp")
    chip, core = lax.div(me, 2), lax.rem(me, 2)
    side = lax.rem(dp, 2)

    def dev(chip_off, other_core=0):
        c = core if isinstance(other_core, int) and other_core == 0 else lax.rem(core + other_core, 2)
        return 2 * lax.rem(chip + chip_off + chips, chips) + c

    right, left, far = dev(1), dev(-1), dev(2)
    sib = 2 * chip + (1 - core)
    to_right, to_left = {"dp": dp, "fsdp": right}, {"dp": dp, "fsdp": left}
    to_pair = {"dp": dp + 1 - 2 * side, "fsdp": me}
    to_sib = {"dp": dp, "fsdp": sib}

    barrier = pltpu.get_barrier_semaphore()
    for target in (to_right, to_left, to_pair, to_sib):
        pl.semaphore_signal(barrier, inc=1, device_id=target, device_id_type=MESH)
    pl.semaphore_wait(barrier, 4)

    kinds = []
    for own, land, rows in ((w_in_ref, g_in, width), (w_out_ref, g_out, out_rows)):
        outer, middle = part_rows(rows)
        kinds.append((own, land, outer, middle))

    def region(kind, part, k, chunks=1):
        _, _, outer, middle = kinds[kind]
        if part == 1:
            rows = middle // CHUNKS
            return aligned(outer + k * rows, 8), rows * chunks
        rows = outer // CHUNKS
        where = side if part == 0 else 1 - side
        return aligned(where * (outer + middle) + k * rows, 8), rows * chunks

    def remote(kind, src, slot, layer, off, rows, ssem, rsem, target):
        _, land, _, _ = kinds[kind]
        source = src.at[layer] if slot is None else src.at[layer, slot]
        return pltpu.make_async_remote_copy(
            src_ref=source.at[pl.ds(off, rows)],
            dst_ref=land.at[layer, me if slot is None else slot, pl.ds(off, rows)],
            send_sem=ssem, recv_sem=rsem, device_id=target, device_id_type=MESH,
        )

    def arrival(kind, layer, slot, off, rows, rsem):
        _, land, _, _ = kinds[kind]
        ref = land.at[layer, slot, pl.ds(off, rows)]
        return pltpu.make_async_remote_copy(
            src_ref=ref, dst_ref=ref, send_sem=sd.at[0], recv_sem=rsem,
            device_id=to_sib, device_id_type=MESH,
        )

    def send_x(g):
        w, i = lax.div(g, items), lax.rem(g, items)
        layer = lax.div(w, 2)
        k = lax.rem(i, CHUNKS)
        for kind in range(2):
            own, land, _, _ = kinds[kind]

            @pl.when(lax.rem(w, 2) == kind)
            def _():
                for stage in range(3):
                    @pl.when(lax.div(i, CHUNKS) == stage)
                    def _():
                        for way, (target, rsem) in enumerate(((to_right, rx), (to_left, rm))):
                            ssem = send.at[w, 3 * way + stage]
                            if stage < 2:
                                off, rows = region(kind, stage, k)
                                remote(kind, own, None, layer, off, rows, ssem, rsem.at[g], target).start()
                            else:
                                off, rows = region(kind, way, k)
                                slot = left if way == 0 else right
                                remote(kind, land, slot, layer, off, rows, ssem, rsem.at[g], target).start()

    def tick(g):
        w, i = lax.div(g, items), lax.rem(g, items)
        layer = lax.div(w, 2)
        k = lax.rem(i, CHUNKS)
        for kind in range(2):
            _, land, _, _ = kinds[kind]

            @pl.when(lax.rem(w, 2) == kind)
            def _():
                for stage in range(3):
                    @pl.when(lax.div(i, CHUNKS) == stage)
                    def _():
                        for way, rsem in enumerate((rx, rm)):
                            slot = far if stage == 2 else (left if way == 0 else right)
                            off, rows = region(kind, way if stage == 2 else stage, k)
                            arrival(kind, layer, slot, off, rows, rsem.at[g]).wait_recv()
                        off, rows = region(kind, 0, k)
                        if stage == 0:
                            for n, slot in enumerate((left, right)):
                                remote(kind, land, slot, layer, off, rows, send.at[w, 6 + n], rp.at[w, n], to_pair).start()
                        if stage == 2:
                            remote(kind, land, far, layer, off, rows, send.at[w, 8], rp.at[w, 2], to_pair).start()

        @pl.when(g + AHEAD < total)
        def _():
            send_x(g + AHEAD)

    def ticks(lo, hi):
        loop(jnp.minimum(lo, total), jnp.minimum(hi, total), tick)

    def take_pair(kind, layer, n):
        off, rows = region(kind, 2, 0, CHUNKS)
        slot = (left, right, far)[n]
        arrival(kind, layer, slot, off, rows, rp.at[2 * layer + kind, n]).wait_recv()

    def sib_send(kind, layer, n):
        own, land, outer, middle = kinds[kind]
        w = 2 * layer + kind
        src, slot = (own, None) if n == 0 else (land, (None, left, right, far)[n])
        remote(kind, src, slot, layer, 0, 2 * outer + middle, sd.at[w, n], rd.at[w, n], to_sib).start()

    def sib_slot(n):
        return (sib, dev(-1, 1), dev(1, 1), dev(2, 1))[n]

    def take_sib(kind, layer, n):
        _, _, outer, middle = kinds[kind]
        ref = kinds[kind][1].at[layer, sib_slot(n)]
        pltpu.make_async_remote_copy(
            src_ref=ref, dst_ref=ref, send_sem=sd.at[2 * layer + kind, n], recv_sem=rd.at[2 * layer + kind, n],
            device_id=to_sib, device_id_type=MESH,
        ).wait_recv()

    def shard_at(s):
        off = jnp.where(s < 2, 0, jnp.where(s >= 6, 2, jnp.where(lax.rem(s, 2) == 0, -1, 1)))
        flip = jnp.where((s == 1) | (s == 4) | (s == 5) | (s == 7), 1, 0)
        return 2 * lax.rem(chip + off + chips, chips) + lax.rem(core + flip, 2)

    def normalise(layer):
        gain = gain_ref[layer].astype(jnp.float32)

        def block(b):
            rows = pl.ds(aligned(b * 128, 128), 128)
            hidden = acc[rows, :].astype(jnp.bfloat16).astype(jnp.float32)
            acc[rows, :] = hidden
            centred = hidden - jnp.mean(hidden, axis=-1, keepdims=True)
            variance = jnp.mean(centred * centred, axis=-1, keepdims=True)
            h[rows, :] = (centred * lax.rsqrt(variance + NORM_EPS) * gain).astype(jnp.bfloat16)

        loop(0, seq // 128, block)

    def in_shard(layer, s):
        d = shard_at(s)
        odd = lax.rem(d, 2)
        base = d * cols - odd * (cols % 128)

        def fetch(j, slot):
            window = pl.ds(aligned(j * TILE, TILE), TILE)

            @pl.when(s == 0)
            def _():
                pltpu.make_async_copy(w_in_ref.at[layer, :, window], wbuf.at[slot], wsem.at[slot]).start()

            @pl.when(s > 0)
            def _():
                pltpu.make_async_copy(g_in.at[layer, d, :, window], wbuf.at[slot], wsem.at[slot]).start()

        tail_window = pl.ds(n_full * TILE, tail)

        @pl.when(s == 0)
        def _():
            pltpu.make_async_copy(w_in_ref.at[layer, :, tail_window], wtail, tsem).start()

        @pl.when(s > 0)
        def _():
            pltpu.make_async_copy(g_in.at[layer, d, :, tail_window], wtail, tsem).start()

        def multiply(weights, n, col):
            shift = cols % 128
            padded = -(-(n + shift) // 128) * 128

            def block(b):
                rows = pl.ds(aligned(b * ROWS, ROWS), ROWS)
                out = jnp.dot(h[rows, :], weights[...], preferred_element_type=jnp.float32).astype(jnp.bfloat16)

                @pl.when(odd == 0)
                def _():
                    proj.at[rows, pl.ds(aligned(base + col, 128), -(-n // 128) * 128)][:, :n] = out

                @pl.when(odd == 1)
                def _():
                    proj.at[rows, pl.ds(aligned(base + col, 128), padded)][:, shift:shift + n] = out

            loop(0, seq // ROWS, block)

        fetch(0, 0)

        def full(j):
            slot = lax.rem(j, 2)

            @pl.when(j + 1 < n_full)
            def _():
                fetch(j + 1, 1 - slot)

            pltpu.make_async_copy(g_in.at[0, 0, :, pl.ds(0, TILE)], wbuf.at[slot], wsem.at[slot]).wait()
            multiply(wbuf.at[slot], TILE, j * TILE)

        loop(0, n_full, full)
        pltpu.make_async_copy(g_in.at[0, 0, :, tail_window], wtail, tsem).wait()
        multiply(wtail, tail, n_full * TILE)

    def rotate(a, rows):
        cos, sin = cos_ref[rows, :], sin_ref[rows, :]
        first, second = a[:, :half], a[:, half:]
        return jnp.concatenate([first * cos - second * sin, second * cos + first * sin], axis=-1)

    q_block = 256

    def keys(layer):
        def block(b):
            rows = pl.ds(aligned(b * q_block, q_block), q_block)
            key = proj[rows, q_cols:q_cols + HEAD_DIM].astype(jnp.float32)
            kbuf[rows, :] = rotate(key, rows).astype(jnp.bfloat16)
            vbuf[rows, :] = proj[rows, q_cols + HEAD_DIM:q_cols + 2 * HEAD_DIM]

        loop(0, seq // q_block, block)
        pltpu.make_async_copy(kbuf, k_ref.at[layer, 0], kvsem.at[0]).start()
        pltpu.make_async_copy(vbuf, v_ref.at[layer, 0], kvsem.at[1]).start()

    blocks = seq // q_block
    shift_cols = 2 * HEAD_DIM

    def attend(t):
        head = heads - 1 - lax.div(t, blocks)
        b = lax.rem(t, blocks)
        rows = pl.ds(aligned(b * q_block, q_block), q_block)
        q = proj[rows, pl.ds(aligned(head * HEAD_DIM, HEAD_DIM), HEAD_DIM)].astype(jnp.float32)
        q = (rotate(q, rows) * HEAD_DIM ** -0.5).astype(jnp.bfloat16)
        s = lax.dot_general(q, kbuf[...], (((1,), (1,)), ((), ())), preferred_element_type=jnp.float32)
        row = b * q_block + lax.broadcasted_iota(jnp.int32, s.shape, 0)
        s = jnp.where(row >= lax.broadcasted_iota(jnp.int32, s.shape, 1), s, -1e30)
        e = jnp.exp(s - jnp.max(s, axis=-1, keepdims=True))
        o = jnp.dot(e.astype(jnp.bfloat16), vbuf[...], preferred_element_type=jnp.float32)
        o = o / jnp.sum(e, axis=-1, keepdims=True)
        proj[rows, pl.ds(aligned(head * HEAD_DIM + shift_cols, HEAD_DIM), HEAD_DIM)] = o.astype(jnp.bfloat16)

    gate0 = q_cols + 2 * HEAD_DIM
    up0 = gate0 + ff

    def gated(t):
        def block(b):
            rows = pl.ds(aligned(b * 256, 256), 256)
            gate_cols = pl.ds(aligned(gate0 + t * TILE, 128), TILE)
            gate = proj[rows, gate_cols].astype(jnp.float32)
            up = proj[rows, pl.ds(aligned(up0 + t * TILE, 128), TILE)].astype(jnp.float32)
            proj[rows, gate_cols] = (jax.nn.silu(gate) * up).astype(jnp.bfloat16)

        loop(0, seq // 256, block)

    n_out = width // TILE

    def out_shard(layer, s):
        d = shard_at(s)

        def fetch(n, slot):
            window = pl.ds(aligned(n * TILE, TILE), TILE)
            target = wbuf.at[slot, pl.ds(0, out_rows)]

            @pl.when(s == 0)
            def _():
                pltpu.make_async_copy(w_out_ref.at[layer, :, window], target, wsem.at[slot]).start()

            @pl.when(s > 0)
            def _():
                pltpu.make_async_copy(g_out.at[layer, d, :, window], target, wsem.at[slot]).start()

        fetch(0, 0)
        left_cols = pl.ds(aligned(shift_cols + d * out_rows, 128), out_rows)

        def tile(n):
            slot = lax.rem(n, 2)

            @pl.when(n + 1 < n_out)
            def _():
                fetch(n + 1, 1 - slot)

            target = wbuf.at[slot, pl.ds(0, out_rows)]
            pltpu.make_async_copy(g_out.at[0, 0, :, pl.ds(0, TILE)], target, wsem.at[slot]).wait()

            def block(b):
                rows = pl.ds(aligned(b * ROWS, ROWS), ROWS)
                window = pl.ds(aligned(n * TILE, TILE), TILE)
                acc[rows, window] += jnp.dot(
                    proj[rows, left_cols], wbuf[slot, :out_rows, :], preferred_element_type=jnp.float32
                )

            loop(0, seq // ROWS, block)

        loop(0, n_out, tile)

    loop(0, AHEAD, send_x)
    copy = pltpu.make_async_copy(x_ref.at[0], h, ysem)
    copy.start()
    copy.wait()

    def widen(b):
        rows = pl.ds(aligned(b * 128, 128), 128)
        acc[rows, :] = h[rows, :].astype(jnp.float32)

    loop(0, seq // 128, widen)

    def layer_step(layer):
        g0 = 2 * items * layer
        sib_send(0, layer, 0)
        sib_send(1, layer, 0)
        normalise(layer)

        def in_step(s):
            lo = jnp.where(s == 1, 1, jnp.where(s == 2, 2, s + 7))
            hi = jnp.where(s == 0, 1, jnp.where(s == 1, 2, s + 8))
            lo = jnp.where(s == 0, 1, lo)
            ticks(g0 + lo, g0 + hi)

            @pl.when(s == 1)
            def _():
                take_sib(0, layer, 0)

            @pl.when(s == 2)
            def _():
                for n in (0, 1):
                    take_pair(0, layer, n)
                    sib_send(0, layer, n + 1)

            for n in (0, 1, 2):
                @pl.when(s == (4, 5, 7)[n])
                def _():
                    take_sib(0, layer, n + 1)

            @pl.when(s == 6)
            def _():
                take_pair(0, layer, 2)
                sib_send(0, layer, 3)

            in_shard(layer, s)

        loop(0, 8, in_step)
        keys(layer)

        def attend_step(t):
            @pl.when(lax.rem(t, 8) == 0)
            def _():
                ticks(g0 + 15 + lax.div(t, 8), g0 + 16 + lax.div(t, 8))
            attend(t)

        loop(0, heads * blocks, attend_step)

        def gated_step(t):
            @pl.when(lax.rem(t, 8) == 0)
            def _():
                ticks(g0 + 19 + lax.div(t, 8), g0 + 20 + lax.div(t, 8))
            gated(t)

        loop(0, ff // TILE, gated_step)

        def out_step(s):
            lo = jnp.where(s == 0, 21, jnp.where(s == 2, 22, jnp.where(s == 3, 23, 24)))
            hi = jnp.where((s == 0) | (s == 2) | (s == 3) | (s == 6), lo + 1, lo)
            ticks(g0 + lo, g0 + hi)

            @pl.when(s == 1)
            def _():
                take_sib(1, layer, 0)

            @pl.when(s == 2)
            def _():
                for n in (0, 1):
                    take_pair(1, layer, n)
                    sib_send(1, layer, n + 1)

            for n in (0, 1, 2):
                @pl.when(s == (4, 5, 7)[n])
                def _():
                    take_sib(1, layer, n + 1)

            @pl.when(s == 6)
            def _():
                take_pair(1, layer, 2)
                sib_send(1, layer, 3)

            out_shard(layer, s)

        loop(0, 8, out_step)
        pltpu.make_async_copy(kbuf, k_ref.at[layer, 0], kvsem.at[0]).wait()
        pltpu.make_async_copy(vbuf, v_ref.at[layer, 0], kvsem.at[1]).wait()

    tick(0)
    loop(0, layers, layer_step)

    def narrow(b):
        rows = pl.ds(aligned(b * 128, 128), 128)
        h[rows, :] = acc[rows, :].astype(jnp.bfloat16)

    loop(0, seq // 128, narrow)
    copy = pltpu.make_async_copy(h, y_ref.at[0], ysem)
    copy.start()

    def drain(layer):
        for kind in range(2):
            _, land, outer, middle = kinds[kind]
            w = 2 * layer + kind
            for n in range(9):
                rows = middle if n in (1, 4, 5) else outer
                ref = land.at[layer, 0, pl.ds(0, rows)]
                pltpu.make_async_remote_copy(
                    src_ref=ref, dst_ref=ref, send_sem=send.at[w, n], recv_sem=rx.at[0],
                    device_id=to_sib, device_id_type=MESH,
                ).wait_send()
            for n in range(4):
                ref = land.at[layer, 0]
                pltpu.make_async_remote_copy(
                    src_ref=ref, dst_ref=ref, send_sem=sd.at[w, n], recv_sem=rx.at[0],
                    device_id=to_sib, device_id_type=MESH,
                ).wait_send()

    loop(0, layers, drain)
    copy.wait()


def solution(mesh):
    batch_axes = ("dp", "fsdp")
    groups, group = mesh.shape["dp"], mesh.shape["fsdp"]

    def device_program(x, gain, w_in, w_out):
        layers, width, cols = w_in.shape
        out_rows = w_out.shape[1]
        seq = x.shape[1]
        total_cols = cols * group
        tail = cols % TILE
        items = 3 * CHUNKS * 2 * layers
        cos, sin = rope_tables(seq)
        any_spec = pl.BlockSpec(memory_space=pl.ANY)
        vmem_spec = pl.BlockSpec(memory_space=pltpu.VMEM)
        bf16, f32 = jnp.bfloat16, jnp.float32
        dma = pltpu.SemaphoreType.DMA
        out = pl.pallas_call(
            functools.partial(kernel, groups, group),
            out_shape=(
                jax.ShapeDtypeStruct(x.shape, bf16),
                jax.ShapeDtypeStruct((layers, 1, seq, HEAD_DIM), bf16),
                jax.ShapeDtypeStruct((layers, 1, seq, HEAD_DIM), bf16),
                jax.ShapeDtypeStruct((layers, group, width, cols), bf16),
                jax.ShapeDtypeStruct((layers, group, out_rows, width), bf16),
            ),
            in_specs=[any_spec, vmem_spec, vmem_spec, vmem_spec, any_spec, any_spec],
            out_specs=[any_spec] * 5,
            scratch_shapes=[
                pltpu.VMEM((seq, width), bf16),
                pltpu.VMEM((seq, width), f32),
                pltpu.VMEM((seq, total_cols), bf16),
                pltpu.VMEM((seq, HEAD_DIM), bf16),
                pltpu.VMEM((seq, HEAD_DIM), bf16),
                pltpu.VMEM((2, width, TILE), bf16),
                pltpu.VMEM((width, tail), bf16),
                dma((items,)),
                dma((items,)),
                dma((2 * layers, 3)),
                dma((2 * layers, 4)),
                dma((2 * layers, 9)),
                dma((2 * layers, 4)),
                dma((2,)),
                dma,
                dma,
                dma((2,)),
            ],
            compiler_params=pltpu.CompilerParams(
                collective_id=0, has_side_effects=True, vmem_limit_bytes=67_043_328
            ),
        )(x, gain.reshape(layers, 1, width), cos, sin, w_in, w_out)
        return out[:3]

    return jax.shard_map(
        device_program,
        mesh=mesh,
        in_specs=(P(batch_axes, None, None), P(None, None), P(None, None, "fsdp"), P(None, "fsdp", None)),
        out_specs=(P(batch_axes, None, None), P(None, batch_axes, None, None), P(None, batch_axes, None, None)),
        check_vma=False,
    )
```

time: 1150 us -> 775 us (0.67)
  Pallas kernels: 0 us -> 737 us
  waiting for transfers between devices: 660 us -> 0 us
  matrix products: 370 us -> 0 us
  other arithmetic: 65.6 us -> 0 us
  between operations: 14.4 us -> 0.64 us
    pallas_call x0 -> x1, Pallas kernels: none -> 737 us  [device_program(): pl.pallas_call(functools.partial(kernel, groups, group), out_shape=(jax.S...]
    all_gather x4 -> x0, waiting for transfers between devices: 659 us -> none  [the longest x2 595 us: device_program(): w_in_full = lax.all_gather(w_in_local[layer], 'fsdp', axis=1, tiled=True)]
    dot_general x10 -> x0, matrix products: 370 us -> none  [the longest x2 186 us: parallel_layer(): jnp.einsum('bsd,de->bse', normed, w_in_full, preferred_element_type=jnp.f...]
    reduce_sum x5 -> x0, other arithmetic: 34.9 us -> none  [the longest x2 27.4 us: mix_tokens(): row_sum = jnp.sum(exp_scores, axis=-1, keepdims=True)]
    slice x4 -> x0, local copies, waits for them, and re-layouts: 26.7 us -> none  [the longest x1 15.5 us: device_program(): w_in_full = lax.all_gather(w_in_local[layer], 'fsdp', axis=1, tiled=True)]
    unnamed x44 -> x4, local copies, waits for them, and re-layouts: 11.8 us -> 34.5 us
  transfers between devices with their start and end apart: 4 -> 0, of which waited for: 4 -> 0; matrix products, arithmetic and copies ran while one was open for 35% -> 0% of each run, Pallas kernels for 0% -> 0%
where the time goes in v1:
time: 775 us; the launch traced here: 773 us
  Pallas kernels  737 us (95%)
  local copies, waits for them, and re-layouts  35.8 us (5%)
    pallas_call x1, Pallas kernels, device_program(): pl.pallas_call(functools.partial(kernel, groups, group), out_shape=(jax.S...  737 us
    unnamed x4, local copies, waits for them, and re-layouts  34.5 us

profile of v1, /device:TPU:113, one launch (start us, length us, event | category | flops | bytes accessed | tf_op | source)
XLA Modules:
  0.0 773.2 jit_solution(3707916089742068998)
XLA Ops:
  0.6 1.3 copy.10.gain_ref
  1.9 25.2 %copy.11.w_in_ref = bf16[2,2048,2368]{2,1,0:T(8,128)(2,1)} copy(bf16[2,2048,2368]{1,2,0:T(8,128)(2,1)} %param.8) | data formatting | bytes 38797312 | tf_op args[2]
  27.1 736.7 %shard_map.85 = (bf16[1,1024,2048]{2,1,0:T(8,128)(2,1)}, bf16[2,1,1024,256]{3,2,1,0:T(8,128)(2,1)}, bf16[2,1,1024,256]{3,2,1,0:T(8,128)(2,1)}, bf16[2,8,2048,236...) custom-call(bf16[1,1024,2048]{2,1,0:T(8,128)(2,1)} %x_ref.1, bf16[2,1,2048]{2,1,0:T(2,128)(2,1)} %copy.10.gain_ref, ...), custom_call_target="tpu_custom_call" | custom-call | tf_op jit(solution)/shard_map/pallas_call | solution.py:497
  763.9 4.8 copy.15
  768.6 2.3 copy.16
  770.9 2.3 copy.17

commit v2 on v1

--- a/solution.py
+++ b/solution.py
@@ -13,7 +13,6 @@
 NORM_EPS = 1e-6
 MESH = pl.DeviceIdType.MESH
 TILE = 512
-ROWS = 512
 CHUNKS = 4
 AHEAD = 4
 
@@ -26,7 +25,7 @@
 
 def part_rows(rows):
     step = 8 * CHUNKS
-    outer = rows // (3 * step) * step
+    outer = round(rows / (3 * step)) * step
     return outer, rows - 2 * outer
 
 
@@ -41,10 +40,10 @@
 def kernel(
     groups, group, x_ref, gain_ref, cos_ref, sin_ref, w_in_ref, w_out_ref,
     y_ref, k_ref, v_ref, g_in, g_out,
-    h, acc, proj, kbuf, vbuf, wbuf, wtail,
+    h, acc, proj, kbuf, vbuf, wbuf, wtail, obuf,
     rx, rm, rp, rd, send, sd, wsem, tsem, ysem, kvsem,
 ):
-    layers, width, cols = w_in_ref.shape
+    layers, cols, width = w_in_ref.shape
     out_rows = w_out_ref.shape[1]
     seq = x_ref.shape[1]
     rows_total = out_rows * group
@@ -53,7 +52,8 @@
     heads = q_cols // HEAD_DIM
     chips = group // 2
     n_full = cols // TILE
-    tail = cols - n_full * TILE
+    rest = (cols - n_full * TILE) // 128 * 128
+    edge = cols - n_full * TILE - rest
     half = HEAD_DIM // 2
     items = 3 * CHUNKS
     total = items * 2 * layers
@@ -79,18 +79,20 @@
     pl.semaphore_wait(barrier, 4)
 
     kinds = []
-    for own, land, rows in ((w_in_ref, g_in, width), (w_out_ref, g_out, out_rows)):
+    for own, land, rows in ((w_in_ref, g_in, cols), (w_out_ref, g_out, out_rows)):
         outer, middle = part_rows(rows)
         kinds.append((own, land, outer, middle))
 
-    def region(kind, part, k, chunks=1):
+    def part_at(kind, part):
         _, _, outer, middle = kinds[kind]
         if part == 1:
-            rows = middle // CHUNKS
-            return aligned(outer + k * rows, 8), rows * chunks
-        rows = outer // CHUNKS
+            return outer, middle
         where = side if part == 0 else 1 - side
-        return aligned(where * (outer + middle) + k * rows, 8), rows * chunks
+        return where * (outer + middle), outer
+
+    def region(kind, part, k):
+        start, rows = part_at(kind, part)
+        return aligned(start + k * (rows // CHUNKS), 8), rows // CHUNKS
 
     def remote(kind, src, slot, layer, off, rows, ssem, rsem, target):
         _, land, _, _ = kinds[kind]
@@ -119,7 +121,7 @@
             @pl.when(lax.rem(w, 2) == kind)
             def _():
                 for stage in range(3):
-                    @pl.when(lax.div(i, CHUNKS) == stage)
+                    @pl.when((lax.div(i, CHUNKS) == stage))
                     def _():
                         for way, (target, rsem) in enumerate(((to_right, rx), (to_left, rm))):
                             ssem = send.at[w, 3 * way + stage]
@@ -141,7 +143,7 @@
             @pl.when(lax.rem(w, 2) == kind)
             def _():
                 for stage in range(3):
-                    @pl.when(lax.div(i, CHUNKS) == stage)
+                    @pl.when((lax.div(i, CHUNKS) == stage))
                     def _():
                         for way, rsem in enumerate((rx, rm)):
                             slot = far if stage == 2 else (left if way == 0 else right)
@@ -162,22 +164,33 @@
         loop(jnp.minimum(lo, total), jnp.minimum(hi, total), tick)
 
     def take_pair(kind, layer, n):
-        off, rows = region(kind, 2, 0, CHUNKS)
+        off, rows = part_at(kind, 2)
+        off = aligned(off, 8)
         slot = (left, right, far)[n]
         arrival(kind, layer, slot, off, rows, rp.at[2 * layer + kind, n]).wait_recv()
+
+    def sib_rows(kind, n):
+        _, _, outer, middle = kinds[kind]
+        if n < 3:
+            return 0, 2 * outer + middle
+        if n == 3:
+            return aligned(side * outer, 8), outer + middle
+        off, rows = part_at(kind, 2)
+        return aligned(off, 8), rows
 
     def sib_send(kind, layer, n):
         own, land, outer, middle = kinds[kind]
         w = 2 * layer + kind
-        src, slot = (own, None) if n == 0 else (land, (None, left, right, far)[n])
-        remote(kind, src, slot, layer, 0, 2 * outer + middle, sd.at[w, n], rd.at[w, n], to_sib).start()
+        src, slot = (own, None) if n == 0 else (land, (None, left, right, far, far)[n])
+        off, rows = sib_rows(kind, n)
+        remote(kind, src, slot, layer, off, rows, sd.at[w, n], rd.at[w, n], to_sib).start()
 
     def sib_slot(n):
-        return (sib, dev(-1, 1), dev(1, 1), dev(2, 1))[n]
+        return (sib, dev(-1, 1), dev(1, 1), dev(2, 1), dev(2, 1))[n]
 
     def take_sib(kind, layer, n):
-        _, _, outer, middle = kinds[kind]
-        ref = kinds[kind][1].at[layer, sib_slot(n)]
+        off, rows = sib_rows(kind, n)
+        ref = kinds[kind][1].at[layer, sib_slot(n), pl.ds(off, rows)]
         pltpu.make_async_remote_copy(
             src_ref=ref, dst_ref=ref, send_sem=sd.at[2 * layer + kind, n], recv_sem=rd.at[2 * layer + kind, n],
             device_id=to_sib, device_id_type=MESH,
@@ -188,8 +201,13 @@
         flip = jnp.where((s == 1) | (s == 4) | (s == 5) | (s == 7), 1, 0)
         return 2 * lax.rem(chip + off + chips, chips) + lax.rem(core + flip, 2)
 
+    def primed(s):
+        return (s == 1) | (s == 3) | (s == 5)
+
     def normalise(layer):
-        gain = gain_ref[layer].astype(jnp.float32)
+        gains = gain_ref[...].astype(jnp.float32)
+        chosen = lax.broadcasted_iota(jnp.int32, gains.shape, 0) == layer
+        gain = jnp.sum(jnp.where(chosen, gains, 0.0), axis=0, keepdims=True)
 
         def block(b):
             rows = pl.ds(aligned(b * 128, 128), 128)
@@ -204,62 +222,59 @@
     def in_shard(layer, s):
         d = shard_at(s)
         odd = lax.rem(d, 2)
-        base = d * cols - odd * (cols % 128)
-
-        def fetch(j, slot):
-            window = pl.ds(aligned(j * TILE, TILE), TILE)
-
+        first = odd * edge
+        base = aligned(d * cols + first, 128)
+
+        def fetch(start, rows, target, sem, s=s, d=d):
             @pl.when(s == 0)
             def _():
-                pltpu.make_async_copy(w_in_ref.at[layer, :, window], wbuf.at[slot], wsem.at[slot]).start()
+                pltpu.make_async_copy(w_in_ref.at[layer, pl.ds(aligned(start, 8), rows)], target, sem).start()
 
             @pl.when(s > 0)
             def _():
-                pltpu.make_async_copy(g_in.at[layer, d, :, window], wbuf.at[slot], wsem.at[slot]).start()
-
-        tail_window = pl.ds(n_full * TILE, tail)
-
-        @pl.when(s == 0)
+                pltpu.make_async_copy(g_in.at[layer, d, pl.ds(aligned(start, 8), rows)], target, sem).start()
+
+        def product(weights):
+            return lax.dot_general(
+                h[...], weights, (((1,), (1,)), ((), ())), preferred_element_type=jnp.float32
+            ).astype(jnp.bfloat16)
+
+        @pl.when(jnp.logical_not(primed(s)))
         def _():
-            pltpu.make_async_copy(w_in_ref.at[layer, :, tail_window], wtail, tsem).start()
-
-        @pl.when(s > 0)
-        def _():
-            pltpu.make_async_copy(g_in.at[layer, d, :, tail_window], wtail, tsem).start()
-
-        def multiply(weights, n, col):
-            shift = cols % 128
-            padded = -(-(n + shift) // 128) * 128
-
-            def block(b):
-                rows = pl.ds(aligned(b * ROWS, ROWS), ROWS)
-                out = jnp.dot(h[rows, :], weights[...], preferred_element_type=jnp.float32).astype(jnp.bfloat16)
-
-                @pl.when(odd == 0)
-                def _():
-                    proj.at[rows, pl.ds(aligned(base + col, 128), -(-n // 128) * 128)][:, :n] = out
-
-                @pl.when(odd == 1)
-                def _():
-                    proj.at[rows, pl.ds(aligned(base + col, 128), padded)][:, shift:shift + n] = out
-
-            loop(0, seq // ROWS, block)
-
-        fetch(0, 0)
+            fetch(first, TILE, wbuf.at[0], wsem.at[0])
+
+        fetch(first + n_full * TILE, rest, wtail.at[pl.ds(0, rest)], tsem.at[0])
+        fetch((1 - odd) * (n_full * TILE + rest), edge, wtail.at[pl.ds(rest, edge)], tsem.at[1])
 
         def full(j):
             slot = lax.rem(j, 2)
 
             @pl.when(j + 1 < n_full)
             def _():
-                fetch(j + 1, 1 - slot)
-
-            pltpu.make_async_copy(g_in.at[0, 0, :, pl.ds(0, TILE)], wbuf.at[slot], wsem.at[slot]).wait()
-            multiply(wbuf.at[slot], TILE, j * TILE)
+                fetch(first + (j + 1) * TILE, TILE, wbuf.at[1 - slot], wsem.at[1 - slot])
+
+            @pl.when((j + 1 == n_full) & primed(s + 1))
+            def _():
+                ahead = shard_at(s + 1)
+                fetch(lax.rem(ahead, 2) * edge, TILE, wbuf.at[n_full % 2], wsem.at[n_full % 2], s + 1, ahead)
+
+            pltpu.make_async_copy(g_in.at[0, 0, pl.ds(0, TILE)], wbuf.at[slot], wsem.at[slot]).wait()
+            proj[:, pl.ds(aligned(base + j * TILE, 128), TILE)] = product(wbuf[slot])
 
         loop(0, n_full, full)
-        pltpu.make_async_copy(g_in.at[0, 0, :, tail_window], wtail, tsem).wait()
-        multiply(wtail, tail, n_full * TILE)
+        pltpu.make_async_copy(g_in.at[0, 0, pl.ds(0, rest)], wtail.at[pl.ds(0, rest)], tsem.at[0]).wait()
+        pltpu.make_async_copy(g_in.at[0, 0, pl.ds(0, edge)], wtail.at[pl.ds(rest, edge)], tsem.at[1]).wait()
+        last = product(wtail[...])
+        proj[:, pl.ds(aligned(base + n_full * TILE, 128), rest)] = last[:, :rest]
+        edges = proj.at[:, pl.ds(aligned(jnp.where(odd == 1, base - 128, base + n_full * TILE + rest), 128), 128)]
+
+        @pl.when(odd == 0)
+        def _():
+            edges[:, :edge] = last[:, rest:]
+
+        @pl.when(odd == 1)
+        def _():
+            edges[:, 128 - edge:] = last[:, rest:]
 
     def rotate(a, rows):
         cos, sin = cos_ref[rows, :], sin_ref[rows, :]
@@ -283,18 +298,26 @@
     shift_cols = 2 * HEAD_DIM
 
     def attend(t):
-        head = heads - 1 - lax.div(t, blocks)
+        two = heads // 2 - 1 - lax.div(t, blocks)
         b = lax.rem(t, blocks)
         rows = pl.ds(aligned(b * q_block, q_block), q_block)
-        q = proj[rows, pl.ds(aligned(head * HEAD_DIM, HEAD_DIM), HEAD_DIM)].astype(jnp.float32)
-        q = (rotate(q, rows) * HEAD_DIM ** -0.5).astype(jnp.bfloat16)
-        s = lax.dot_general(q, kbuf[...], (((1,), (1,)), ((), ())), preferred_element_type=jnp.float32)
-        row = b * q_block + lax.broadcasted_iota(jnp.int32, s.shape, 0)
-        s = jnp.where(row >= lax.broadcasted_iota(jnp.int32, s.shape, 1), s, -1e30)
-        e = jnp.exp(s - jnp.max(s, axis=-1, keepdims=True))
-        o = jnp.dot(e.astype(jnp.bfloat16), vbuf[...], preferred_element_type=jnp.float32)
-        o = o / jnp.sum(e, axis=-1, keepdims=True)
-        proj[rows, pl.ds(aligned(head * HEAD_DIM + shift_cols, HEAD_DIM), HEAD_DIM)] = o.astype(jnp.bfloat16)
+        q = proj[rows, pl.ds(aligned(two * 2 * HEAD_DIM, 2 * HEAD_DIM), 2 * HEAD_DIM)].astype(jnp.float32)
+        q = jnp.concatenate([rotate(q[:, :HEAD_DIM], rows), rotate(q[:, HEAD_DIM:], rows)], axis=0)
+        q = (q * HEAD_DIM ** -0.5).astype(jnp.bfloat16)
+        for n in range(blocks):
+            @pl.when(b == n)
+            def _():
+                seen = (n + 1) * q_block
+                s = lax.dot_general(q, kbuf[:seen, :], (((1,), (1,)), ((), ())), preferred_element_type=jnp.float32)
+                own = s[:, n * q_block:]
+                row = lax.broadcasted_iota(jnp.int32, own.shape, 0) & (q_block - 1)
+                own = jnp.where(row >= lax.broadcasted_iota(jnp.int32, own.shape, 1), own, -1e30)
+                s = own if n == 0 else jnp.concatenate([s[:, :n * q_block], own], axis=1)
+                e = jnp.exp(s - jnp.max(s, axis=-1, keepdims=True))
+                o = jnp.dot(e.astype(jnp.bfloat16), vbuf[:seen, :], preferred_element_type=jnp.float32)
+                o = (o / jnp.sum(e, axis=-1, keepdims=True)).astype(jnp.bfloat16)
+                place = pl.ds(aligned(two * 2 * HEAD_DIM + shift_cols, 2 * HEAD_DIM), 2 * HEAD_DIM)
+                proj[rows, place] = jnp.concatenate([o[:q_block], o[q_block:]], axis=1)
 
     gate0 = q_cols + 2 * HEAD_DIM
     up0 = gate0 + ff
@@ -314,9 +337,9 @@
     def out_shard(layer, s):
         d = shard_at(s)
 
-        def fetch(n, slot):
+        def fetch(n, slot, s=s, d=d):
             window = pl.ds(aligned(n * TILE, TILE), TILE)
-            target = wbuf.at[slot, pl.ds(0, out_rows)]
+            target = obuf.at[slot]
 
             @pl.when(s == 0)
             def _():
@@ -326,7 +349,10 @@
             def _():
                 pltpu.make_async_copy(g_out.at[layer, d, :, window], target, wsem.at[slot]).start()
 
-        fetch(0, 0)
+        @pl.when(jnp.logical_not(primed(s)))
+        def _():
+            fetch(0, 0)
+
         left_cols = pl.ds(aligned(shift_cols + d * out_rows, 128), out_rows)
 
         def tile(n):
@@ -336,17 +362,13 @@
             def _():
                 fetch(n + 1, 1 - slot)
 
-            target = wbuf.at[slot, pl.ds(0, out_rows)]
-            pltpu.make_async_copy(g_out.at[0, 0, :, pl.ds(0, TILE)], target, wsem.at[slot]).wait()
-
-            def block(b):
-                rows = pl.ds(aligned(b * ROWS, ROWS), ROWS)
-                window = pl.ds(aligned(n * TILE, TILE), TILE)
-                acc[rows, window] += jnp.dot(
-                    proj[rows, left_cols], wbuf[slot, :out_rows, :], preferred_element_type=jnp.float32
-                )
-
-            loop(0, seq // ROWS, block)
+            @pl.when((n + 1 == n_out) & primed(s + 1))
+            def _():
+                fetch(0, n_out % 2, s + 1, shard_at(s + 1))
+
+            pltpu.make_async_copy(g_out.at[0, 0, :, pl.ds(0, TILE)], obuf.at[slot], wsem.at[slot]).wait()
+            window = pl.ds(aligned(n * TILE, TILE), TILE)
+            acc[:, window] += jnp.dot(proj[:, left_cols], obuf[slot], preferred_element_type=jnp.float32)
 
         loop(0, n_out, tile)
 
@@ -367,13 +389,19 @@
         sib_send(1, layer, 0)
         normalise(layer)
 
+        def run_ticks(s, start, ends):
+            lo, hi = start, ends[0]
+            for n in range(1, len(ends)):
+                lo = jnp.where(s == n, ends[n - 1], lo)
+                hi = jnp.where(s == n, ends[n], hi)
+            ticks(g0 + lo, g0 + hi)
+
         def in_step(s):
-            lo = jnp.where(s == 1, 1, jnp.where(s == 2, 2, s + 7))
-            hi = jnp.where(s == 0, 1, jnp.where(s == 1, 2, s + 8))
-            lo = jnp.where(s == 0, 1, lo)
-            ticks(g0 + lo, g0 + hi)
-
-            @pl.when(s == 1)
+            n = 3 * CHUNKS
+            ends = (1, 2, 10, 11, 12, 13, 14, 15)
+            run_ticks(s, 1, ends)
+
+            @pl.when(s == 0)
             def _():
                 take_sib(0, layer, 0)
 
@@ -383,15 +411,20 @@
                     take_pair(0, layer, n)
                     sib_send(0, layer, n + 1)
 
-            for n in (0, 1, 2):
-                @pl.when(s == (4, 5, 7)[n])
+            for first, at in ((1, 4), (3, 7)):
+                @pl.when(s == at)
                 def _():
-                    take_sib(0, layer, n + 1)
+                    take_sib(0, layer, first)
+                    take_sib(0, layer, first + 1)
+
+            @pl.when(s == 5)
+            def _():
+                sib_send(0, layer, 3)
 
             @pl.when(s == 6)
             def _():
                 take_pair(0, layer, 2)
-                sib_send(0, layer, 3)
+                sib_send(0, layer, 4)
 
             in_shard(layer, s)
 
@@ -399,27 +432,24 @@
         keys(layer)
 
         def attend_step(t):
-            @pl.when(lax.rem(t, 8) == 0)
-            def _():
-                ticks(g0 + 15 + lax.div(t, 8), g0 + 16 + lax.div(t, 8))
+            @pl.when(lax.rem(t, 4) == 2)
+            def _():
+                n = g0 + 15 + lax.div(t, 4)
+                ticks(n, n + 1)
             attend(t)
 
-        loop(0, heads * blocks, attend_step)
+        loop(0, heads // 2 * blocks, attend_step)
 
         def gated_step(t):
-            @pl.when(lax.rem(t, 8) == 0)
-            def _():
-                ticks(g0 + 19 + lax.div(t, 8), g0 + 20 + lax.div(t, 8))
             gated(t)
 
         loop(0, ff // TILE, gated_step)
 
         def out_step(s):
-            lo = jnp.where(s == 0, 21, jnp.where(s == 2, 22, jnp.where(s == 3, 23, 24)))
-            hi = jnp.where((s == 0) | (s == 2) | (s == 3) | (s == 6), lo + 1, lo)
-            ticks(g0 + lo, g0 + hi)
-
-            @pl.when(s == 1)
+            n = 6 * CHUNKS
+            run_ticks(s, 19, (20, 21, 22, 22, 23, 24, 25, 25))
+
+            @pl.when(s == 0)
             def _():
                 take_sib(1, layer, 0)
 
@@ -429,15 +459,20 @@
                     take_pair(1, layer, n)
                     sib_send(1, layer, n + 1)
 
-            for n in (0, 1, 2):
-                @pl.when(s == (4, 5, 7)[n])
+            for first, at in ((1, 4), (3, 7)):
+                @pl.when(s == at)
                 def _():
-                    take_sib(1, layer, n + 1)
+                    take_sib(1, layer, first)
+                    take_sib(1, layer, first + 1)
 
             @pl.when(s == 6)
             def _():
+                sib_send(1, layer, 3)
+
+            @pl.when(s == 6)
+            def _():
                 take_pair(1, layer, 2)
-                sib_send(1, layer, 3)
+                sib_send(1, layer, 4)
 
             out_shard(layer, s)
 
@@ -451,10 +486,10 @@
     def narrow(b):
         rows = pl.ds(aligned(b * 128, 128), 128)
         h[rows, :] = acc[rows, :].astype(jnp.bfloat16)
+        pltpu.make_async_copy(h.at[rows], y_ref.at[0, rows], ysem).start()
 
     loop(0, seq // 128, narrow)
     copy = pltpu.make_async_copy(h, y_ref.at[0], ysem)
-    copy.start()
 
     def drain(layer):
         for kind in range(2):
@@ -467,8 +502,8 @@
                     src_ref=ref, dst_ref=ref, send_sem=send.at[w, n], recv_sem=rx.at[0],
                     device_id=to_sib, device_id_type=MESH,
                 ).wait_send()
-            for n in range(4):
-                ref = land.at[layer, 0]
+            for n in range(5):
+                ref = land.at[layer, 0, pl.ds(0, sib_rows(kind, n)[1])]
                 pltpu.make_async_remote_copy(
                     src_ref=ref, dst_ref=ref, send_sem=sd.at[w, n], recv_sem=rx.at[0],
                     device_id=to_sib, device_id_type=MESH,
@@ -483,7 +518,8 @@
     groups, group = mesh.shape["dp"], mesh.shape["fsdp"]
 
     def device_program(x, gain, w_in, w_out):
-        layers, width, cols = w_in.shape
+        w_in = jnp.swapaxes(w_in, 1, 2)
+        layers, cols, width = w_in.shape
         out_rows = w_out.shape[1]
         seq = x.shape[1]
         total_cols = cols * group
@@ -500,7 +536,7 @@
                 jax.ShapeDtypeStruct(x.shape, bf16),
                 jax.ShapeDtypeStruct((layers, 1, seq, HEAD_DIM), bf16),
                 jax.ShapeDtypeStruct((layers, 1, seq, HEAD_DIM), bf16),
-                jax.ShapeDtypeStruct((layers, group, width, cols), bf16),
+                jax.ShapeDtypeStruct((layers, group, cols, width), bf16),
                 jax.ShapeDtypeStruct((layers, group, out_rows, width), bf16),
             ),
             in_specs=[any_spec, vmem_spec, vmem_spec, vmem_spec, any_spec, any_spec],
@@ -511,23 +547,24 @@
                 pltpu.VMEM((seq, total_cols), bf16),
                 pltpu.VMEM((seq, HEAD_DIM), bf16),
                 pltpu.VMEM((seq, HEAD_DIM), bf16),
-                pltpu.VMEM((2, width, TILE), bf16),
-                pltpu.VMEM((width, tail), bf16),
+                pltpu.VMEM((2, TILE, width), bf16),
+                pltpu.VMEM((tail, width), bf16),
+                pltpu.VMEM((2, out_rows, TILE), bf16),
                 dma((items,)),
                 dma((items,)),
                 dma((2 * layers, 3)),
-                dma((2 * layers, 4)),
+                dma((2 * layers, 5)),
                 dma((2 * layers, 9)),
-                dma((2 * layers, 4)),
+                dma((2 * layers, 5)),
                 dma((2,)),
-                dma,
+                dma((2,)),
                 dma,
                 dma((2,)),
             ],
             compiler_params=pltpu.CompilerParams(
                 collective_id=0, has_side_effects=True, vmem_limit_bytes=67_043_328
             ),
-        )(x, gain.reshape(layers, 1, width), cos, sin, w_in, w_out)
+        )(x, gain, cos, sin, w_in, w_out)
         return out[:3]
 
     return jax.shard_map(

time: 775 us -> 706 us (0.911)
  Pallas kernels: 737 us -> 695 us
  local copies, waits for them, and re-layouts: 35.8 us -> 8.11 us
    pallas_call x1, Pallas kernels: 737 us -> 695 us  [device_program(): pl.pallas_call(functools.partial(kernel, groups, group), out_shape=(jax.S...]
    unnamed x4 -> x5, local copies, waits for them, and re-layouts: 34.5 us -> 8.11 us
where the time goes in v2:
time: 706 us; the launch traced here: 704 us
  Pallas kernels  695 us (98%)
  local copies, waits for them, and re-layouts  8.11 us (1%)
    pallas_call x1, Pallas kernels, device_program(): pl.pallas_call(functools.partial(kernel, groups, group), out_shape=(jax.S...  695 us

profile of v2, /device:TPU:113, one launch (start us, length us, event | category | flops | bytes accessed | tf_op | source)
XLA Modules:
  0.0 704.0 jit_solution(3068225914684941891)
XLA Ops:
  0.6 695.3 %shard_map.85 = (bf16[1,1024,2048]{2,1,0:T(8,128)(2,1)}, bf16[2,1,1024,256]{3,2,1,0:T(8,128)(2,1)}, bf16[2,1,1024,256]{3,2,1,0:T(8,128)(2,1)}, bf16[2,8,2368,204...) custom-call(bf16[1,1024,2048]{2,1,0:T(8,128)(2,1)} %x_ref.1, bf16[2,2048]{1,0:T(2,128)(2,1)} %gain_ref.1, ...), custom_call_target="tpu_custom_call" | custom-call | tf_op jit(solution)/shard_map/pallas_call | solution.py:533
  695.9 0.0 copy-start
  695.9 4.9 copy.12
  700.8 2.3 copy.13
  703.1 0.0 copy-done
  703.1 1.0 copy.14
Async XLA Ops:
  695.9 7.2 %copy-start = (bf16[2,1,1024,256]{3,2,1,0:T(8,128)(2,1)S(1)}, bf16[2,1,1024,256]{3,2,1,0:T(8,128)(2,1)}, u32[]{:S(2)}) copy-start(bf16[2,1,1024,256]{3,2,1,0:T(8,128)(2,1)} %get-tuple-element.14) | copy-start | bytes 3145732

commit v3 on v2

--- a/solution.py
+++ b/solution.py
@@ -370,6 +370,11 @@
             window = pl.ds(aligned(n * TILE, TILE), TILE)
             acc[:, window] += jnp.dot(proj[:, left_cols], obuf[slot], preferred_element_type=jnp.float32)
 
+            @pl.when((layer == layers - 1) & (s == 7))
+            def _():
+                h[:, window] = acc[:, window].astype(jnp.bfloat16)
+                pltpu.make_async_copy(h.at[:, window], y_ref.at[0, :, window], ysem).start()
+
         loop(0, n_out, tile)
 
     loop(0, AHEAD, send_x)
@@ -417,7 +422,7 @@
                     take_sib(0, layer, first)
                     take_sib(0, layer, first + 1)
 
-            @pl.when(s == 5)
+            @pl.when(s == 4)
             def _():
                 sib_send(0, layer, 3)
 
@@ -447,7 +452,7 @@
 
         def out_step(s):
             n = 6 * CHUNKS
-            run_ticks(s, 19, (20, 21, 22, 22, 23, 24, 25, 25))
+            run_ticks(s, 19, (21, 22, 22, 23, 24, 24, 25, 25))
 
             @pl.when(s == 0)
             def _():
@@ -465,7 +470,7 @@
                     take_sib(1, layer, first)
                     take_sib(1, layer, first + 1)
 
-            @pl.when(s == 6)
+            @pl.when(s == 5)
             def _():
                 sib_send(1, layer, 3)
 
@@ -483,12 +488,6 @@
     tick(0)
     loop(0, layers, layer_step)
 
-    def narrow(b):
-        rows = pl.ds(aligned(b * 128, 128), 128)
-        h[rows, :] = acc[rows, :].astype(jnp.bfloat16)
-        pltpu.make_async_copy(h.at[rows], y_ref.at[0, rows], ysem).start()
-
-    loop(0, seq // 128, narrow)
     copy = pltpu.make_async_copy(h, y_ref.at[0], ysem)
 
     def drain(layer):

time: 706 us -> 705 us (level)
  no operation moved by 1% of the time
where the time goes in v3:
time: 705 us
  Pallas kernels  696 us (99%)
  local copies, waits for them, and re-layouts  8.11 us (1%)
    pallas_call x1, Pallas kernels, device_program(): pl.pallas_call(functools.partial(kernel, groups, group), out_shape=(jax.S...  696 us

profile of v3, /device:TPU:113, one launch (start us, length us, event | category | flops | bytes accessed | tf_op | source)
XLA Modules:
  0.0 704.7 jit_solution(5978962328303113113)
XLA Ops:
  0.6 695.9 %shard_map.85 = (bf16[1,1024,2048]{2,1,0:T(8,128)(2,1)}, bf16[2,1,1024,256]{3,2,1,0:T(8,128)(2,1)}, bf16[2,1,1024,256]{3,2,1,0:T(8,128)(2,1)}, bf16[2,8,2368,204...) custom-call(bf16[1,1024,2048]{2,1,0:T(8,128)(2,1)} %x_ref.1, bf16[2,2048]{1,0:T(2,128)(2,1)} %gain_ref.1, ...), custom_call_target="tpu_custom_call" | custom-call | tf_op jit(solution)/shard_map/pallas_call | solution.py:532
  696.6 0.0 copy-start
  696.6 4.9 copy.12
  701.5 2.3 copy.13
  703.7 0.0 copy-done
  703.7 1.0 copy.14
Async XLA Ops:
  696.6 7.2 %copy-start = (bf16[2,1,1024,256]{3,2,1,0:T(8,128)(2,1)S(1)}, bf16[2,1,1024,256]{3,2,1,0:T(8,128)(2,1)}, u32[]{:S(2)}) copy-start(bf16[2,1,1024,256]{3,2,1,0:T(8,128)(2,1)} %get-tuple-element.14) | copy-start | bytes 3145732
